TPU v7x, 32 devices: a whole 2x2x4 slice. The times are simulated.
32 devices in a mesh: groups: 2 (over y), seq: 4 (over z), head: 2 (over x), inner: 2 (over core).
Axes of the slice: x: 2, y: 2, z: 4, core: 2. Of those that a mesh axis runs over, the one named last changes fastest.
Arguments:
- queries: bfloat16 [4096, 2, 8, 128], P(('groups', 'seq'), 'head', 'inner'), parts along dimension 0, may hold values from -120 to 120
- grad_out: bfloat16 [4096, 2, 8, 128], P(('groups', 'seq'), 'head', 'inner'), parts along dimension 0, may hold values from -6 to 6
- keys: bfloat16 [4096, 2, 128], P(('groups', 'seq'), 'head'), parts along dimension 0, may hold values from -6 to 6
- values: bfloat16 [4096, 2, 128], P(('groups', 'seq'), 'head'), parts along dimension 0, may hold values from -6 to 6
- indices: int32 [2, 64, 16], P('head', 'groups'), parts along dimension 1, may hold values from 0 to 31, as said below
- valid: int32 [2, 64, 16], P('head', 'groups'), parts along dimension 1, may hold values from 0 to 1
Outputs:
- grad_queries: bfloat16 [4096, 2, 8, 128], P(('groups', 'seq'), 'head', 'inner'), parts along dimension 0
- grad_keys: bfloat16 [4096, 2, 128], P(('groups', 'seq'), 'head'), parts along dimension 0
- grad_values: bfloat16 [4096, 2, 128], P(('groups', 'seq'), 'head'), parts along dimension 0
There are 2 independent parts, one for each index of `groups`. A program takes and returns all parts, laid end to end along the dimension named above; each array names one. Nothing has to cross between parts.
Inputs may be any that keep to these rules, and one draw needn't show every extreme that they name: `indices`: call blocks r * 8 to r * 8 + 7 run r. For every KV head and query block b: slot 0 names b and is valid; the valid slots name distinct blocks at most b; over all query blocks of run r, the valid slots name blocks of runs later than r never, and for each earlier run exactly 4 distinct blocks of it. Slots that are not valid name arbitrary blocks.
All inputs are finite; a program needn't handle non-finite values.
Results may differ from a plain program's by a relative error of at most 0.007.
Values may be sent and summed in bfloat16 or wider, within the bound.
No kernel may reach another device: no remote copies, remote signals or barrier semaphores. Data moves between devices by JAX's collectives and lax.ppermute only.
A program may use at most 64 MiB of HBM per device.

v0:
```python
import math
import jax
import jax.numpy as jnp
from jax import lax
from jax.sharding import PartitionSpec as P

BLK = 64
TOPK = 16
CAP = 4


def per_device(queries, grad_out, keys, values, indices, valid):
    tokens = queries.shape[0]
    heads_here = queries.shape[2]
    width = queries.shape[3]
    seq_count = lax.axis_size("seq")
    seq_here = lax.axis_index("seq")
    blocks_here = tokens // BLK
    total_blocks = indices.shape[1]
    scaling = 1.0 / math.sqrt(width)
    remote_rows = seq_count * CAP
    dest_rows = remote_rows + blocks_here
    picks_all = indices[0]
    valid_all = valid[0] > 0
    owner_all = picks_all // blocks_here
    local_all = picks_all % blocks_here
    my_picks = lax.dynamic_slice_in_dim(picks_all, seq_here * blocks_here, blocks_here, 0)
    my_valid = lax.dynamic_slice_in_dim(valid_all, seq_here * blocks_here, blocks_here, 0)
    my_owner = my_picks // blocks_here
    my_local = my_picks % blocks_here
    remote = my_valid & (my_owner != seq_here)
    block_ids = jnp.arange(total_blocks, dtype=jnp.int32)
    hits_in = (my_picks[:, :, None] == block_ids[None, None, :]) & remote[:, :, None]
    present_in = jnp.any(hits_in, axis=(0, 1)).reshape(seq_count, blocks_here)
    rank_in = jnp.cumsum(present_in.astype(jnp.int32), axis=1) - 1
    slot_ref = jnp.sum(jnp.where(hits_in, rank_in.reshape(-1)[None, None, :], 0), axis=2)
    row_index = jnp.where(remote, my_owner * CAP + slot_ref, remote_rows + my_local)
    source_run = block_ids // blocks_here
    incoming = valid_all & (owner_all == seq_here) & (source_run != seq_here)[:, None]
    hits_out = (
        local_all[:, :, None] == jnp.arange(blocks_here, dtype=jnp.int32)[None, None, :]
    ) & incoming[:, :, None]
    present_out = jnp.any(hits_out.reshape(seq_count, blocks_here * TOPK, blocks_here), axis=1)
    rank_out = jnp.cumsum(present_out.astype(jnp.int32), axis=1) - 1
    choose_out = present_out[:, None, :] & (
        rank_out[:, None, :] == jnp.arange(CAP, dtype=jnp.int32)[None, :, None]
    )
    wanted = my_picks.reshape(-1)
    blank = jnp.zeros((blocks_here * TOPK, BLK, width), jnp.bfloat16)
    carry = (blank, blank)
    key_piece = lax.all_gather(keys, "seq", axis=0, tiled=True)
    value_piece = lax.all_gather(values, "seq", axis=0, tiled=True)
    count = key_piece.shape[0] // BLK
    relative = wanted
    inside = (relative >= 0) & (relative < count)
    relative = jnp.clip(relative, 0, count - 1)
    key_rows = jnp.take(key_piece[:, 0].reshape(count, BLK, width), relative, axis=0)
    value_rows = jnp.take(value_piece[:, 0].reshape(count, BLK, width), relative, axis=0)
    sel_keys = jnp.where(inside[:, None, None], key_rows, carry[0])
    sel_values = jnp.where(inside[:, None, None], value_rows, carry[1])
    group = math.gcd(blocks_here, max(1, 512 // (BLK * heads_here)))
    steps_count = blocks_here // group
    span = TOPK * BLK
    position = jnp.arange(BLK, dtype=jnp.int32)
    causal = position[None, :] <= position[:, None]
    block_global = seq_here * blocks_here + jnp.arange(blocks_here, dtype=jnp.int32)
    before = my_picks < block_global[:, None]
    same = my_picks == block_global[:, None]
    allowed = my_valid[:, None, :, None] & (
        before[:, None, :, None] | same[:, None, :, None] & causal[None, :, None, :]
    )
    allowed = allowed.reshape(steps_count, group, BLK, span)
    query_steps = queries[:, 0].reshape(steps_count, group, BLK, heads_here, width)
    grad_steps = grad_out[:, 0].reshape(steps_count, group, BLK, heads_here, width)
    key_steps = sel_keys.reshape(steps_count, group, span, width)
    value_steps = sel_values.reshape(steps_count, group, span, width)
    row_steps = row_index.reshape(steps_count, group * TOPK)

    def attend(carry, inputs):
        key_acc, value_acc = carry
        q_group, do_group, k_group, v_group, mask_group, rows_group = inputs
        mask_heads = mask_group[:, None, :, :]
        scores = (
            jnp.einsum("qigw,qsw->qgis", q_group, k_group, preferred_element_type=jnp.float32)
            * scaling
        )
        highest = jnp.max(jnp.where(mask_heads, scores, -jnp.inf), axis=-1, keepdims=True)
        weights = jnp.where(mask_heads, jnp.exp(scores - highest), 0.0)
        probs = weights / jnp.sum(weights, axis=-1, keepdims=True)
        probs_b = probs.astype(jnp.bfloat16)
        dprobs = jnp.einsum("qigw,qsw->qgis", do_group, v_group, preferred_element_type=jnp.float32)
        delta = jnp.sum(probs * dprobs, axis=-1, keepdims=True)
        dscores = (probs * (dprobs - delta)).astype(jnp.bfloat16)
        query_grad = (
            jnp.einsum("qgis,qsw->qigw", dscores, k_group, preferred_element_type=jnp.float32)
            * scaling
        ).astype(jnp.bfloat16)
        key_terms = (
            jnp.einsum("qgis,qigw->qsw", dscores, q_group, preferred_element_type=jnp.float32)
            * scaling
        )
        value_terms = jnp.einsum(
            "qgis,qigw->qsw", probs_b, do_group, preferred_element_type=jnp.float32
        )
        key_acc = key_acc.at[rows_group].add(key_terms.reshape(group * TOPK, BLK * width))
        value_acc = value_acc.at[rows_group].add(value_terms.reshape(group * TOPK, BLK * width))
        return ((key_acc, value_acc), query_grad)

    zeros_dest = jnp.zeros((dest_rows, BLK * width), jnp.float32)
    (key_acc, value_acc), query_grads = lax.scan(
        attend,
        (zeros_dest, zeros_dest),
        (query_steps, grad_steps, key_steps, value_steps, allowed, row_steps),
    )
    grad_queries = query_grads.reshape(tokens, 1, heads_here, width)
    send_key_tiles = key_acc[:remote_rows].reshape(seq_count, CAP, BLK * width)
    send_value_tiles = value_acc[:remote_rows].reshape(seq_count, CAP, BLK * width)
    own_keys = key_acc[remote_rows:]
    own_values = value_acc[remote_rows:]
    choose_float = choose_out.astype(jnp.float32)
    back_keys, back_values = (
        lax.all_to_all(send_key_tiles, "seq", split_axis=0, concat_axis=0, tiled=True),
        lax.all_to_all(send_value_tiles, "seq", split_axis=0, concat_axis=0, tiled=True),
    )
    local_keys = own_keys + jnp.einsum(
        "dcb,dcx->bx", choose_float, back_keys, precision=lax.Precision.HIGHEST
    )
    local_values = own_values + jnp.einsum(
        "dcb,dcx->bx", choose_float, back_values, precision=lax.Precision.HIGHEST
    )
    total_keys, total_values = lax.psum((local_keys, local_values), "inner")
    grad_keys = total_keys.astype(jnp.bfloat16).reshape(tokens, 1, width)
    grad_values = total_values.astype(jnp.bfloat16).reshape(tokens, 1, width)
    return (grad_queries, grad_keys, grad_values)


def solution(mesh):
    return jax.shard_map(
        per_device,
        mesh=mesh,
        in_specs=(
            P(("groups", "seq"), "head", "inner", None),
            P(("groups", "seq"), "head", "inner", None),
            P(("groups", "seq"), "head", None),
            P(("groups", "seq"), "head", None),
            P("head", "groups", None),
            P("head", "groups", None),
        ),
        out_specs=(
            P(("groups", "seq"), "head", "inner", None),
            P(("groups", "seq"), "head", None),
            P(("groups", "seq"), "head", None),
        ),
        check_vma=False,
    )
```

profile of v0, /device:TPU:0, one launch (start us, length us, event | category | flops | bytes accessed | tf_op | source)
XLA Modules:
  0.0 166.9 jit_solution(11409170172867323838)
XLA Ops:
  4.3 17.6 %all_gather.6 = bf16[2048,1,128]{2,0,1:T(8,128)(2,1)S(1)} all-gather(bf16[512,1,128]{2,0,1:T(8,128)(2,1)} %param.12), channel_id=1, replica_groups=mesh['groups'=2,'seq'=4,'head'=2,'inner'=2] {'seq'}, dimensions={0}, use_global_device_ids=true | all-gather | bytes 655360 | tf_op jit(solution)/shard_map/all_gather | solution.py:51
  21.9 16.6 %all_gather.7 = bf16[2048,1,128]{2,0,1:T(8,128)(2,1)S(1)} all-gather(bf16[512,1,128]{2,0,1:T(8,128)(2,1)} %param.13), channel_id=1, replica_groups=mesh['groups'=2,'seq'=4,'head'=2,'inner'=2] {'seq'}, dimensions={0}, use_global_device_ids=true | all-gather | bytes 655360 | tf_op jit(solution)/shard_map/all_gather | solution.py:52
  38.5 1.0 gather_fusion.1
  39.4 2.1 %gather_fusion = bf16[128,64,128]{2,1,0:T(8,128)(2,1)} fusion(bf16[32,64,128]{2,1,0:T(8,128)(2,1)S(1)} %bitcast.131, s32[1024]{0:T(1024)S(1)} %pad_clamp_fusion), kind=kCustom, calls=%fused_computation.clone | custom fusion | bytes 4194816 | tf_op jit(solution)/shard_map/jit(_take)/gather | solution.py:57
  41.6 1.2 or_and_fusion
  42.8 3.7 %select_select_fusion = (bf16[128,64,128]{2,1,0:T(8,128)(2,1)}, bf16[128,64,128]{2,1,0:T(8,128)(2,1)}) fusion(bf16[128,64,128]{2,1,0:T(8,128)(2,1)S(1)} %gather_fusion.1, pred[128]{0:T(512)(128)(4,1)S(1)} %compare_and_fusion.2, pred[128]{0:T(512)(128)(4,1)S(1)} %and.166, bf16[128,64,128]{2,1,0:T(8,128)(2,1)} %gather_fusion), kind=kLoop, calls=%fused_computation.54 | loop fusion | flops 4194304 | bytes 8388864 | tf_op jit(solution)/shard_map/jit(_where)/select_n | solution.py:60
  46.6 84.0 %while.14 = (s32[]{:T(128)}, f32[24,8192]{1,0:T(8,128)S(1)}, f32[24,8192]{1,0:T(8,128)S(1)}, bf16[4,2,64,4,128]{4,3,2,1,0:T(4,128)(2,1)}, s32[4,32]{1,0:T(4,128)...) while((s32[]{:T(128)}, f32[24,8192]{1,0:T(8,128)S(1)}, ...), condition=%wide.region_9.11_spmd, body=%wide.region_3.10_spmd.sunk | while | flops 679871104 | bytes 52703944 | solution.py:110
  46.6 0.9 dynamic-slice_bitcast_fusion.6
  47.5 1.1 constant_dynamic-slice_fusion.4
  48.6 1.5 fusion.74
  50.9 1.3 copy-done
  52.2 1.7 %convolution_bitcast_fusion.5 = f32[2,1024,128]{2,1,0:T(8,128)} fusion(bf16[1,2,64,4,128]{4,3,2,1,0:T(4,128)(2,1)S(1)} %get-tuple-element.196, f32[2,4,64,1024]{3,2,1,0:T(8,128)S(1)} %get-tuple-element.194, f32[2,4,64]{2,1,0:T(4,128)S(1)} %get-tuple-element.195), kind=kOutput, calls=%fused_computation.16.clone.1 | convolution fusion | flops 135266304 | bytes 3278848 | tf_op jit(solution)/shard_map/while/body/eval_jaxpr/qgis,qigw->qsw/dot_general | solution.py:102
  53.9 1.4 reshape.340
  55.3 2.1 %scatter_fusion.1 = f32[24,8192]{1,0:T(8,128)S(1)} fusion(f32[24,8192]{1,0:T(8,128)S(1)} %get-tuple-element.212, s32[32]{0:T(128)S(1)} %fusion.73, f32[32,8192]{1,0:T(8,128)S(1)} %reshape.340), kind=kCustom, calls=%fused_computation.3.clone.1 | custom fusion | flops 262144 | bytes 3145856 | tf_op jit(solution)/shard_map/while/body/eval_jaxpr/scatter-add | solution.py:106
  57.4 2.4 %fusion.76 = (f32[2,4,64]{2,1,0:T(4,128)S(1)}, f32[2,1024,64,4]{1,2,3,0:T(8,128)S(1)}) fusion(f32[2,4,64,1024]{3,2,1,0:T(8,128)} %copy-done, f32[2,4,64]{2,1,0:T(4,128)S(1)} %get-tuple-element.195, bf16[1,2,64,4,128]{4,3,2,1,0:T(4,128)(2,1)S(1)} %get-tuple-element.196, bf16[4,2,1024,128]{3,2,1,0:T(8,128)(2,1)} %get-tuple-element.229, s32[]{:T(128)S(6)} %copy.84), kind=kOutput, calls=%fused_computation.7.clone.1 | convolution fusion | flops 135790080 | bytes 4853764 | tf_op jit(solution)/shard_map/while/body/eval_jaxpr/qigw,qsw->qgis/dot_general | solution.py:91
  60.2 1.5 fusion.79
  61.7 1.5 fusion.78
  63.3 1.4 reshape.339
  64.7 2.1 %scatter_fusion = f32[24,8192]{1,0:T(8,128)S(1)} fusion(f32[24,8192]{1,0:T(8,128)S(1)} %get-tuple-element.211, s32[32]{0:T(128)S(1)} %fusion.73, f32[32,8192]{1,0:T(8,128)S(1)} %reshape.339), kind=kCustom, calls=%fused_computation.2.clone.1 | custom fusion | flops 262144 | bytes 3145856 | tf_op jit(solution)/shard_map/while/body/eval_jaxpr/scatter-add | solution.py:105
  67.6 0.9 dynamic-slice_bitcast_fusion.6
  68.5 1.1 constant_dynamic-slice_fusion.4
  69.6 1.5 fusion.74
  71.9 1.3 copy-done
  73.2 1.7 %convolution_bitcast_fusion.5 = f32[2,1024,128]{2,1,0:T(8,128)} fusion(bf16[1,2,64,4,128]{4,3,2,1,0:T(4,128)(2,1)S(1)} %get-tuple-element.196, f32[2,4,64,1024]{3,2,1,0:T(8,128)S(1)} %get-tuple-element.194, f32[2,4,64]{2,1,0:T(4,128)S(1)} %get-tuple-element.195), kind=kOutput, calls=%fused_computation.16.clone.1 | convolution fusion | flops 135266304 | bytes 3278848 | tf_op jit(solution)/shard_map/while/body/eval_jaxpr/qgis,qigw->qsw/dot_general | solution.py:102
  74.9 1.4 reshape.340
  76.3 2.1 %scatter_fusion.1 = f32[24,8192]{1,0:T(8,128)S(1)} fusion(f32[24,8192]{1,0:T(8,128)S(1)} %get-tuple-element.212, s32[32]{0:T(128)S(1)} %fusion.73, f32[32,8192]{1,0:T(8,128)S(1)} %reshape.340), kind=kCustom, calls=%fused_computation.3.clone.1 | custom fusion | flops 262144 | bytes 3145856 | tf_op jit(solution)/shard_map/while/body/eval_jaxpr/scatter-add | solution.py:106
  78.4 2.4 %fusion.76 = (f32[2,4,64]{2,1,0:T(4,128)S(1)}, f32[2,1024,64,4]{1,2,3,0:T(8,128)S(1)}) fusion(f32[2,4,64,1024]{3,2,1,0:T(8,128)} %copy-done, f32[2,4,64]{2,1,0:T(4,128)S(1)} %get-tuple-element.195, bf16[1,2,64,4,128]{4,3,2,1,0:T(4,128)(2,1)S(1)} %get-tuple-element.196, bf16[4,2,1024,128]{3,2,1,0:T(8,128)(2,1)} %get-tuple-element.229, s32[]{:T(128)S(6)} %copy.84), kind=kOutput, calls=%fused_computation.7.clone.1 | convolution fusion | flops 135790080 | bytes 4853764 | tf_op jit(solution)/shard_map/while/body/eval_jaxpr/qigw,qsw->qgis/dot_general | solution.py:91
  81.2 1.5 fusion.79
  82.7 1.5 fusion.78
  84.3 1.4 reshape.339
  85.7 2.1 %scatter_fusion = f32[24,8192]{1,0:T(8,128)S(1)} fusion(f32[24,8192]{1,0:T(8,128)S(1)} %get-tuple-element.211, s32[32]{0:T(128)S(1)} %fusion.73, f32[32,8192]{1,0:T(8,128)S(1)} %reshape.339), kind=kCustom, calls=%fused_computation.2.clone.1 | custom fusion | flops 262144 | bytes 3145856 | tf_op jit(solution)/shard_map/while/body/eval_jaxpr/scatter-add | solution.py:105
  88.6 0.9 dynamic-slice_bitcast_fusion.6
  89.5 1.1 constant_dynamic-slice_fusion.4
  90.6 1.5 fusion.74
  92.9 1.3 copy-done
  94.2 1.7 %convolution_bitcast_fusion.5 = f32[2,1024,128]{2,1,0:T(8,128)} fusion(bf16[1,2,64,4,128]{4,3,2,1,0:T(4,128)(2,1)S(1)} %get-tuple-element.196, f32[2,4,64,1024]{3,2,1,0:T(8,128)S(1)} %get-tuple-element.194, f32[2,4,64]{2,1,0:T(4,128)S(1)} %get-tuple-element.195), kind=kOutput, calls=%fused_computation.16.clone.1 | convolution fusion | flops 135266304 | bytes 3278848 | tf_op jit(solution)/shard_map/while/body/eval_jaxpr/qgis,qigw->qsw/dot_general | solution.py:102
  95.9 1.4 reshape.340
  97.3 2.1 %scatter_fusion.1 = f32[24,8192]{1,0:T(8,128)S(1)} fusion(f32[24,8192]{1,0:T(8,128)S(1)} %get-tuple-element.212, s32[32]{0:T(128)S(1)} %fusion.73, f32[32,8192]{1,0:T(8,128)S(1)} %reshape.340), kind=kCustom, calls=%fused_computation.3.clone.1 | custom fusion | flops 262144 | bytes 3145856 | tf_op jit(solution)/shard_map/while/body/eval_jaxpr/scatter-add | solution.py:106
  99.4 2.4 %fusion.76 = (f32[2,4,64]{2,1,0:T(4,128)S(1)}, f32[2,1024,64,4]{1,2,3,0:T(8,128)S(1)}) fusion(f32[2,4,64,1024]{3,2,1,0:T(8,128)} %copy-done, f32[2,4,64]{2,1,0:T(4,128)S(1)} %get-tuple-element.195, bf16[1,2,64,4,128]{4,3,2,1,0:T(4,128)(2,1)S(1)} %get-tuple-element.196, bf16[4,2,1024,128]{3,2,1,0:T(8,128)(2,1)} %get-tuple-element.229, s32[]{:T(128)S(6)} %copy.84), kind=kOutput, calls=%fused_computation.7.clone.1 | convolution fusion | flops 135790080 | bytes 4853764 | tf_op jit(solution)/shard_map/while/body/eval_jaxpr/qigw,qsw->qgis/dot_general | solution.py:91
  102.2 1.5 fusion.79
  103.7 1.5 fusion.78
  105.3 1.4 reshape.339
  106.7 2.1 %scatter_fusion = f32[24,8192]{1,0:T(8,128)S(1)} fusion(f32[24,8192]{1,0:T(8,128)S(1)} %get-tuple-element.211, s32[32]{0:T(128)S(1)} %fusion.73, f32[32,8192]{1,0:T(8,128)S(1)} %reshape.339), kind=kCustom, calls=%fused_computation.2.clone.1 | custom fusion | flops 262144 | bytes 3145856 | tf_op jit(solution)/shard_map/while/body/eval_jaxpr/scatter-add | solution.py:105
  109.6 0.9 dynamic-slice_bitcast_fusion.6
  110.5 1.1 constant_dynamic-slice_fusion.4
  111.6 1.5 fusion.74
  113.9 1.3 copy-done
  115.2 1.7 %convolution_bitcast_fusion.5 = f32[2,1024,128]{2,1,0:T(8,128)} fusion(bf16[1,2,64,4,128]{4,3,2,1,0:T(4,128)(2,1)S(1)} %get-tuple-element.196, f32[2,4,64,1024]{3,2,1,0:T(8,128)S(1)} %get-tuple-element.194, f32[2,4,64]{2,1,0:T(4,128)S(1)} %get-tuple-element.195), kind=kOutput, calls=%fused_computation.16.clone.1 | convolution fusion | flops 135266304 | bytes 3278848 | tf_op jit(solution)/shard_map/while/body/eval_jaxpr/qgis,qigw->qsw/dot_general | solution.py:102
  116.9 1.4 reshape.340
  118.3 2.1 %scatter_fusion.1 = f32[24,8192]{1,0:T(8,128)S(1)} fusion(f32[24,8192]{1,0:T(8,128)S(1)} %get-tuple-element.212, s32[32]{0:T(128)S(1)} %fusion.73, f32[32,8192]{1,0:T(8,128)S(1)} %reshape.340), kind=kCustom, calls=%fused_computation.3.clone.1 | custom fusion | flops 262144 | bytes 3145856 | tf_op jit(solution)/shard_map/while/body/eval_jaxpr/scatter-add | solution.py:106
  120.4 2.4 %fusion.76 = (f32[2,4,64]{2,1,0:T(4,128)S(1)}, f32[2,1024,64,4]{1,2,3,0:T(8,128)S(1)}) fusion(f32[2,4,64,1024]{3,2,1,0:T(8,128)} %copy-done, f32[2,4,64]{2,1,0:T(4,128)S(1)} %get-tuple-element.195, bf16[1,2,64,4,128]{4,3,2,1,0:T(4,128)(2,1)S(1)} %get-tuple-element.196, bf16[4,2,1024,128]{3,2,1,0:T(8,128)(2,1)} %get-tuple-element.229, s32[]{:T(128)S(6)} %copy.84), kind=kOutput, calls=%fused_computation.7.clone.1 | convolution fusion | flops 135790080 | bytes 4853764 | tf_op jit(solution)/shard_map/while/body/eval_jaxpr/qigw,qsw->qgis/dot_general | solution.py:91
  123.2 1.5 fusion.79
  124.7 1.5 fusion.78
  126.3 1.4 reshape.339
  127.7 2.1 %scatter_fusion = f32[24,8192]{1,0:T(8,128)S(1)} fusion(f32[24,8192]{1,0:T(8,128)S(1)} %get-tuple-element.211, s32[32]{0:T(128)S(1)} %fusion.73, f32[32,8192]{1,0:T(8,128)S(1)} %reshape.339), kind=kCustom, calls=%fused_computation.2.clone.1 | custom fusion | flops 262144 | bytes 3145856 | tf_op jit(solution)/shard_map/while/body/eval_jaxpr/scatter-add | solution.py:105
  130.6 0.9 reshape.280
  131.5 4.1 %all-to-all-start = ((f32[4,4,8192]{2,1,0:T(4,128)}), f32[4,4,8192]{2,1,0:T(4,128)S(1)}, u32[]{:S(2)}, u32[]{:S(2)}) async-start(f32[4,4,8192]{2,1,0:T(4,128)} %reshape.280), calls=%async_computation | async-start | bytes 1048576 | tf_op jit(solution)/shard_map/all_to_all | solution.py:122
  136.1 1.0 reshape.282
  137.0 8.9 %all-to-all-done = f32[4,4,8192]{2,1,0:T(4,128)S(1)} async-done(((f32[4,4,8192]{2,1,0:T(4,128)}), f32[4,4,8192]{2,1,0:T(4,128)S(1)}, u32[]{:S(2)}, u32[]{:S(2)}) %all-to-all-start) | async-done | bytes 524320 | tf_op jit(solution)/shard_map/all_to_all | solution.py:122
  146.0 3.5 %all-to-all-start.1 = ((f32[4,4,8192]{2,1,0:T(4,128)}), f32[4,4,8192]{2,1,0:T(4,128)S(1)}, u32[]{:S(2)}, u32[]{:S(2)}) async-start(f32[4,4,8192]{2,1,0:T(4,128)} %reshape.282), calls=%async_computation.1 | async-start | bytes 1048576 | tf_op jit(solution)/shard_map/all_to_all | solution.py:123
  149.8 0.9 fusion.30
  150.7 9.0 %all-to-all-done.1 = f32[4,4,8192]{2,1,0:T(4,128)S(1)} async-done(((f32[4,4,8192]{2,1,0:T(4,128)}), f32[4,4,8192]{2,1,0:T(4,128)S(1)}, u32[]{:S(2)}, u32[]{:S(2)}) %all-to-all-start.1) | async-done | bytes 524320 | tf_op jit(solution)/shard_map/all_to_all | solution.py:123
  159.7 0.9 fusion.31
  160.6 4.8 %all-reduce.2 = (bf16[8,8192]{1,0:T(8,128)(2,1)S(1)}, bf16[8,8192]{1,0:T(8,128)(2,1)S(1)}) all-reduce(f32[8,8192]{1,0:T(8,128)S(1)} %fusion.30, f32[8,8192]{1,0:T(8,128)S(1)} %fusion.31), channel_id=1, replica_groups=mesh['groups'=2,'seq'=4,'head'=2,'inner'=2] {'inner'}, use_global_device_ids=true, to_apply=%region_12.14 | all-reduce | flops 131072 | bytes 786432 | tf_op jit(solution)/shard_map/psum | solution.py:131
  (77 shorter events, 14.0 us)
Async XLA Ops:
  50.9 1.3 copy-start
  57.4 2.4 %copy-start.1 = (f32[2,4,64,1024]{3,2,1,0:T(8,128)S(1)}, f32[2,4,64,1024]{3,2,1,0:T(8,128)}, u32[]{:S(2)}) copy-start(f32[2,4,64,1024]{3,2,1,0:T(8,128)} %copy-done) | copy-start | bytes 6291460 | tf_op jit(solution)/shard_map/while
  71.9 1.3 copy-start
  78.4 2.4 %copy-start.1 = (f32[2,4,64,1024]{3,2,1,0:T(8,128)S(1)}, f32[2,4,64,1024]{3,2,1,0:T(8,128)}, u32[]{:S(2)}) copy-start(f32[2,4,64,1024]{3,2,1,0:T(8,128)} %copy-done) | copy-start | bytes 6291460 | tf_op jit(solution)/shard_map/while
  92.9 1.3 copy-start
  99.4 2.4 %copy-start.1 = (f32[2,4,64,1024]{3,2,1,0:T(8,128)S(1)}, f32[2,4,64,1024]{3,2,1,0:T(8,128)}, u32[]{:S(2)}) copy-start(f32[2,4,64,1024]{3,2,1,0:T(8,128)} %copy-done) | copy-start | bytes 6291460 | tf_op jit(solution)/shard_map/while
  113.9 1.3 copy-start
  120.4 2.4 %copy-start.1 = (f32[2,4,64,1024]{3,2,1,0:T(8,128)S(1)}, f32[2,4,64,1024]{3,2,1,0:T(8,128)}, u32[]{:S(2)}) copy-start(f32[2,4,64,1024]{3,2,1,0:T(8,128)} %copy-done) | copy-start | bytes 6291460 | tf_op jit(solution)/shard_map/while
  131.5 14.4 %all-to-all-start = ((f32[4,4,8192]{2,1,0:T(4,128)}), f32[4,4,8192]{2,1,0:T(4,128)S(1)}, u32[]{:S(2)}, u32[]{:S(2)}) async-start(f32[4,4,8192]{2,1,0:T(4,128)} %reshape.280), calls=%async_computation | async-start | bytes 1048576 | tf_op jit(solution)/shard_map/all_to_all | solution.py:122
  146.0 13.7 %all-to-all-start.1 = ((f32[4,4,8192]{2,1,0:T(4,128)}), f32[4,4,8192]{2,1,0:T(4,128)S(1)}, u32[]{:S(2)}, u32[]{:S(2)}) async-start(f32[4,4,8192]{2,1,0:T(4,128)} %reshape.282), calls=%async_computation.1 | async-start | bytes 1048576 | tf_op jit(solution)/shard_map/all_to_all | solution.py:123
where the time goes:
time: 168 us; the launch traced here: 167 us
  blocking collectives  39 us (23%)
  local copies, waits for them, and re-layouts  37.2 us (22%)
  matrix products  36.2 us (22%)
  other arithmetic  27.9 us (17%)
  waiting for transfers between devices  17.9 us (11%)
  starting transfers between devices  7.61 us (5%)
    all_gather x1, blocking collectives, per_device(): key_piece = lax.all_gather(keys, 'seq', axis=0, tiled=True)  17.6 us
    all_gather x1, blocking collectives, per_device(): value_piece = lax.all_gather(values, 'seq', axis=0, tiled=True)  16.6 us
    dot_general x4, matrix products, attend(): jnp.einsum('qigw,qsw->qgis', do_group, v_group, preferred_element_type=jn...  9.67 us
    all_to_all x1, waiting for transfers between devices, per_device(): lax.all_to_all(send_value_tiles, 'seq', split_axis=0, concat_axis=0, tile...  9 us
    all_to_all x1, waiting for transfers between devices, per_device(): lax.all_to_all(send_key_tiles, 'seq', split_axis=0, concat_axis=0, tiled=...  8.93 us
    scatter-add x4, other arithmetic, attend(): key_acc.at[rows_group].add(key_terms.reshape(group * TOPK, BLK * width))  8.42 us
    scatter-add x4, other arithmetic, attend(): value_acc.at[rows_group].add(value_terms.reshape(group * TOPK, BLK * width))  8.42 us
    dot_general x4, matrix products, attend(): jnp.einsum('qgis,qigw->qsw', probs_b, do_group, preferred_element_type=jn...  6.69 us
  transfers between devices with their start and end apart: 2, of which 2 were waited for; matrix products, arithmetic and copies ran while one was open for 2% of the time, Pallas kernels for 0%

commit v1 on v0

--- a/solution.py
+++ b/solution.py
@@ -49,7 +49,14 @@
     blank = jnp.zeros((blocks_here * TOPK, BLK, width), jnp.bfloat16)
     carry = (blank, blank)
     key_piece = lax.all_gather(keys, "seq", axis=0, tiled=True)
-    value_piece = lax.all_gather(values, "seq", axis=0, tiled=True)
+    size = lax.axis_size("seq")
+    right = [(i, (i + 1) % size) for i in range(size)]
+    parts = [values]
+    for far in range(1, size):
+        parts = [lax.ppermute(parts[0], "seq", right), *parts]
+    result = jnp.concatenate(parts, axis=0)
+    shift = (lax.axis_index("seq") + 1) * parts[-1].shape[0]
+    value_piece = jnp.roll(result, shift, axis=0)
     count = key_piece.shape[0] // BLK
     relative = wanted
     inside = (relative >= 0) & (relative < count)

time: 168 us -> 161 us (0.958)
  blocking collectives: 39 us -> 20.4 us
  waiting for transfers between devices: 17.9 us -> 30 us
  local copies, waits for them, and re-layouts: 37.2 us -> 33.7 us
  starting transfers between devices: 7.61 us -> 10.5 us
    all_gather x1 -> x0, blocking collectives: 16.6 us -> none  [per_device(): value_piece = lax.all_gather(values, 'seq', axis=0, tiled=True)]
    ppermute x0 -> x3, waiting for transfers between devices: none -> 12.1 us  [per_device(): parts = [lax.ppermute(parts[0], 'seq', right), *parts]]
    broadcast_in_dim x4, local copies, waits for them, and re-layouts: 3.66 us -> 0.05 us  [attend(): weights = jnp.where(mask_heads, jnp.exp(scores - highest), 0.0)]
    ppermute x0 -> x3, starting transfers between devices: none -> 3.51 us  [per_device(): parts = [lax.ppermute(parts[0], 'seq', right), *parts]]
    all_gather x1, blocking collectives: 17.6 us -> 15.6 us  [per_device(): key_piece = lax.all_gather(keys, 'seq', axis=0, tiled=True)]
  transfers between devices with their start and end apart: 2 -> 5, of which waited for: 2 -> 4; matrix products, arithmetic and copies ran while one was open for 2% -> 5% of each run, Pallas kernels for 0% -> 0%
where the time goes in v1:
time: 161 us; the launch traced here: 160 us
  matrix products  36.2 us (22%)
  local copies, waits for them, and re-layouts  33.7 us (21%)
  waiting for transfers between devices  30 us (19%)
  other arithmetic  27.7 us (17%)
  blocking collectives  20.4 us (13%)
  starting transfers between devices  10.5 us (7%)
    all_gather x1, blocking collectives, per_device(): key_piece = lax.all_gather(keys, 'seq', axis=0, tiled=True)  15.6 us
    ppermute x3, waiting for transfers between devices, per_device(): parts = [lax.ppermute(parts[0], 'seq', right), *parts]  12.1 us
    dot_general x4, matrix products, attend(): jnp.einsum('qigw,qsw->qgis', do_group, v_group, preferred_element_type=jn...  9.67 us
    all_to_all x1, waiting for transfers between devices, per_device(): lax.all_to_all(send_value_tiles, 'seq', split_axis=0, concat_axis=0, tile...  9 us
    all_to_all x1, waiting for transfers between devices, per_device(): lax.all_to_all(send_key_tiles, 'seq', split_axis=0, concat_axis=0, tiled=...  8.89 us
    scatter-add x4, other arithmetic, attend(): value_acc.at[rows_group].add(value_terms.reshape(group * TOPK, BLK * width))  8.42 us
    scatter-add x4, other arithmetic, attend(): key_acc.at[rows_group].add(key_terms.reshape(group * TOPK, BLK * width))  8.42 us
    dot_general x4, matrix products, attend(): jnp.einsum('qgis,qigw->qsw', probs_b, do_group, preferred_element_type=jn...  6.69 us
  transfers between devices with their start and end apart: 5, of which 4 were waited for; matrix products, arithmetic and copies ran while one was open for 5% of the time, Pallas kernels for 0%

profile of v1, /device:TPU:0, one launch (start us, length us, event | category | flops | bytes accessed | tf_op | source)
XLA Modules:
  0.0 159.8 jit_solution(7180185238645311445)
XLA Ops:
  0.6 3.1 %collective-permute-start = (bf16[512,1,128]{2,0,1:T(8,128)(2,1)}, bf16[512,1,128]{2,0,1:T(8,128)(2,1)S(1)}, u32[]{:S(2)}, u32[]{:S(2)}) collective-permute-start(bf16[512,1,128]{2,0,1:T(8,128)(2,1)} %param.13), channel_id=1, source_target_pairs={{0,4},{4,8},{8,12},{12,0},{1,5},{5,9},{9,13},{13,1},{2,6},{6,10},{... | collective-permute-start | bytes 393224 | tf_op jit(solution)/shard_map/ppermute | solution.py:56
  6.4 15.6 %all_gather.3 = bf16[2048,1,128]{2,0,1:T(8,128)(2,1)S(1)} all-gather(bf16[512,1,128]{2,0,1:T(8,128)(2,1)} %param.12), channel_id=1, replica_groups=mesh['groups'=2,'seq'=4,'head'=2,'inner'=2] {'seq'}, dimensions={0}, use_global_device_ids=true | all-gather | bytes 655360 | tf_op jit(solution)/shard_map/all_gather | solution.py:51
  23.0 1.0 gather_fusion
  24.8 6.0 %collective-permute-done.1 = bf16[512,1,128]{2,0,1:T(8,128)(2,1)S(1)} collective-permute-done((bf16[512,1,128]{2,0,1:T(8,128)(2,1)S(1)}, bf16[512,1,128]{2,0,1:T(8,128)(2,1)S(1)}, u32[]{:S(2)}, u32[]{:S(2)}) %collective-permute-start.1) | collective-permute-done | bytes 131104 | tf_op jit(solution)/shard_map/ppermute | solution.py:56
  31.5 6.1 %collective-permute-done.2 = bf16[512,1,128]{2,0,1:T(8,128)(2,1)S(1)} collective-permute-done((bf16[512,1,128]{2,0,1:T(8,128)(2,1)S(1)}, bf16[512,1,128]{2,0,1:T(8,128)(2,1)S(1)}, u32[]{:S(2)}, u32[]{:S(2)}) %collective-permute-start.2) | collective-permute-done | bytes 131104 | tf_op jit(solution)/shard_map/ppermute | solution.py:56
  37.8 2.1 %gather_fusion.1 = bf16[128,64,128]{2,1,0:T(8,128)(2,1)} fusion(bf16[32,64,128]{2,1,0:T(8,128)(2,1)S(1)} %bitcast.132, s32[1024]{0:T(1024)S(1)} %pad_clamp_fusion), kind=kCustom, calls=%fused_computation.1.clone | custom fusion | bytes 4194816 | tf_op jit(solution)/shard_map/jit(_take)/gather | solution.py:65
  40.0 3.7 %select_select_fusion = (bf16[128,64,128]{2,1,0:T(8,128)(2,1)}, bf16[128,64,128]{2,1,0:T(8,128)(2,1)}) fusion(bf16[128,64,128]{2,1,0:T(8,128)(2,1)} %gather_fusion.1, pred[128]{0:T(512)(128)(4,1)S(1)} %compare_and_fusion.2, pred[128]{0:T(512)(128)(4,1)S(1)} %and.172, bf16[128,64,128]{2,1,0:T(8,128)(2,1)S(1)} %gather_fusion), kind=kLoop, calls=%fused_computation.54 | loop fusion | flops 4194304 | bytes 8388864 | tf_op jit(solution)/shard_map/jit(_where)/select_n | solution.py:67
  43.8 80.4 %while.14 = (s32[]{:T(128)}, f32[24,8192]{1,0:T(8,128)S(1)}, f32[24,8192]{1,0:T(8,128)S(1)}, bf16[4,2,64,4,128]{4,3,2,1,0:T(4,128)(2,1)}, s32[4,32]{1,0:T(4,128)...) while((s32[]{:T(128)}, f32[24,8192]{1,0:T(8,128)S(1)}, ...), condition=%wide.region_9.11_spmd, body=%wide.region_3.10_spmd.sunk | while | flops 679871104 | bytes 52703944 | solution.py:117
  43.8 1.1 constant_dynamic-slice_fusion.5
  44.9 1.5 fusion.74
  46.4 0.9 fusion.75
  47.3 1.3 copy-done
  48.6 1.7 %convolution_bitcast_fusion.5 = f32[2,1024,128]{2,1,0:T(8,128)} fusion(bf16[1,2,64,4,128]{4,3,2,1,0:T(4,128)(2,1)S(1)} %get-tuple-element.196, f32[2,4,64,1024]{3,2,1,0:T(8,128)S(1)} %get-tuple-element.194, f32[2,4,64]{2,1,0:T(4,128)S(1)} %get-tuple-element.195), kind=kOutput, calls=%fused_computation.16.clone.1 | convolution fusion | flops 135266304 | bytes 3278848 | tf_op jit(solution)/shard_map/while/body/eval_jaxpr/qgis,qigw->qsw/dot_general | solution.py:109
  50.2 1.4 reshape.340
  51.6 2.1 %scatter_fusion.1 = f32[24,8192]{1,0:T(8,128)S(1)} fusion(f32[24,8192]{1,0:T(8,128)S(1)} %get-tuple-element.212, s32[32]{0:T(128)S(1)} %fusion.73, f32[32,8192]{1,0:T(8,128)S(1)} %reshape.340), kind=kCustom, calls=%fused_computation.3.clone.1 | custom fusion | flops 262144 | bytes 3145856 | tf_op jit(solution)/shard_map/while/body/eval_jaxpr/scatter-add | solution.py:113
  53.8 2.4 %fusion.76 = (f32[2,4,64]{2,1,0:T(4,128)S(1)}, f32[2,1024,64,4]{1,2,3,0:T(8,128)S(1)}) fusion(f32[2,4,64,1024]{3,2,1,0:T(8,128)} %copy-done, f32[2,4,64]{2,1,0:T(4,128)S(1)} %get-tuple-element.195, bf16[1,2,64,4,128]{4,3,2,1,0:T(4,128)(2,1)S(1)} %get-tuple-element.196, bf16[4,2,1024,128]{3,2,1,0:T(8,128)(2,1)} %get-tuple-element.229, s32[]{:T(128)S(6)} %copy.91), kind=kOutput, calls=%fused_computation.7.clone.1 | convolution fusion | flops 135790080 | bytes 4853764 | tf_op jit(solution)/shard_map/while/body/eval_jaxpr/qigw,qsw->qgis/dot_general | solution.py:98
  56.6 1.5 fusion.79
  58.1 1.5 fusion.78
  59.6 1.4 reshape.339
  61.0 2.1 %scatter_fusion = f32[24,8192]{1,0:T(8,128)S(1)} fusion(f32[24,8192]{1,0:T(8,128)S(1)} %get-tuple-element.211, s32[32]{0:T(128)S(1)} %fusion.73, f32[32,8192]{1,0:T(8,128)S(1)} %reshape.339), kind=kCustom, calls=%fused_computation.2.clone.1 | custom fusion | flops 262144 | bytes 3145856 | tf_op jit(solution)/shard_map/while/body/eval_jaxpr/scatter-add | solution.py:112
  63.9 1.1 constant_dynamic-slice_fusion.5
  65.0 1.5 fusion.74
  66.5 0.9 fusion.75
  67.4 1.3 copy-done
  68.6 1.7 %convolution_bitcast_fusion.5 = f32[2,1024,128]{2,1,0:T(8,128)} fusion(bf16[1,2,64,4,128]{4,3,2,1,0:T(4,128)(2,1)S(1)} %get-tuple-element.196, f32[2,4,64,1024]{3,2,1,0:T(8,128)S(1)} %get-tuple-element.194, f32[2,4,64]{2,1,0:T(4,128)S(1)} %get-tuple-element.195), kind=kOutput, calls=%fused_computation.16.clone.1 | convolution fusion | flops 135266304 | bytes 3278848 | tf_op jit(solution)/shard_map/while/body/eval_jaxpr/qgis,qigw->qsw/dot_general | solution.py:109
  70.3 1.4 reshape.340
  71.7 2.1 %scatter_fusion.1 = f32[24,8192]{1,0:T(8,128)S(1)} fusion(f32[24,8192]{1,0:T(8,128)S(1)} %get-tuple-element.212, s32[32]{0:T(128)S(1)} %fusion.73, f32[32,8192]{1,0:T(8,128)S(1)} %reshape.340), kind=kCustom, calls=%fused_computation.3.clone.1 | custom fusion | flops 262144 | bytes 3145856 | tf_op jit(solution)/shard_map/while/body/eval_jaxpr/scatter-add | solution.py:113
  73.9 2.4 %fusion.76 = (f32[2,4,64]{2,1,0:T(4,128)S(1)}, f32[2,1024,64,4]{1,2,3,0:T(8,128)S(1)}) fusion(f32[2,4,64,1024]{3,2,1,0:T(8,128)} %copy-done, f32[2,4,64]{2,1,0:T(4,128)S(1)} %get-tuple-element.195, bf16[1,2,64,4,128]{4,3,2,1,0:T(4,128)(2,1)S(1)} %get-tuple-element.196, bf16[4,2,1024,128]{3,2,1,0:T(8,128)(2,1)} %get-tuple-element.229, s32[]{:T(128)S(6)} %copy.91), kind=kOutput, calls=%fused_computation.7.clone.1 | convolution fusion | flops 135790080 | bytes 4853764 | tf_op jit(solution)/shard_map/while/body/eval_jaxpr/qigw,qsw->qgis/dot_general | solution.py:98
  76.7 1.5 fusion.79
  78.1 1.5 fusion.78
  79.7 1.4 reshape.339
  81.1 2.1 %scatter_fusion = f32[24,8192]{1,0:T(8,128)S(1)} fusion(f32[24,8192]{1,0:T(8,128)S(1)} %get-tuple-element.211, s32[32]{0:T(128)S(1)} %fusion.73, f32[32,8192]{1,0:T(8,128)S(1)} %reshape.339), kind=kCustom, calls=%fused_computation.2.clone.1 | custom fusion | flops 262144 | bytes 3145856 | tf_op jit(solution)/shard_map/while/body/eval_jaxpr/scatter-add | solution.py:112
  84.0 1.1 constant_dynamic-slice_fusion.5
  85.1 1.5 fusion.74
  86.6 0.9 fusion.75
  87.4 1.3 copy-done
  88.7 1.7 %convolution_bitcast_fusion.5 = f32[2,1024,128]{2,1,0:T(8,128)} fusion(bf16[1,2,64,4,128]{4,3,2,1,0:T(4,128)(2,1)S(1)} %get-tuple-element.196, f32[2,4,64,1024]{3,2,1,0:T(8,128)S(1)} %get-tuple-element.194, f32[2,4,64]{2,1,0:T(4,128)S(1)} %get-tuple-element.195), kind=kOutput, calls=%fused_computation.16.clone.1 | convolution fusion | flops 135266304 | bytes 3278848 | tf_op jit(solution)/shard_map/while/body/eval_jaxpr/qgis,qigw->qsw/dot_general | solution.py:109
  90.4 1.4 reshape.340
  91.8 2.1 %scatter_fusion.1 = f32[24,8192]{1,0:T(8,128)S(1)} fusion(f32[24,8192]{1,0:T(8,128)S(1)} %get-tuple-element.212, s32[32]{0:T(128)S(1)} %fusion.73, f32[32,8192]{1,0:T(8,128)S(1)} %reshape.340), kind=kCustom, calls=%fused_computation.3.clone.1 | custom fusion | flops 262144 | bytes 3145856 | tf_op jit(solution)/shard_map/while/body/eval_jaxpr/scatter-add | solution.py:113
  93.9 2.4 %fusion.76 = (f32[2,4,64]{2,1,0:T(4,128)S(1)}, f32[2,1024,64,4]{1,2,3,0:T(8,128)S(1)}) fusion(f32[2,4,64,1024]{3,2,1,0:T(8,128)} %copy-done, f32[2,4,64]{2,1,0:T(4,128)S(1)} %get-tuple-element.195, bf16[1,2,64,4,128]{4,3,2,1,0:T(4,128)(2,1)S(1)} %get-tuple-element.196, bf16[4,2,1024,128]{3,2,1,0:T(8,128)(2,1)} %get-tuple-element.229, s32[]{:T(128)S(6)} %copy.91), kind=kOutput, calls=%fused_computation.7.clone.1 | convolution fusion | flops 135790080 | bytes 4853764 | tf_op jit(solution)/shard_map/while/body/eval_jaxpr/qigw,qsw->qgis/dot_general | solution.py:98
  96.7 1.5 fusion.79
  98.2 1.5 fusion.78
  99.8 1.4 reshape.339
  101.2 2.1 %scatter_fusion = f32[24,8192]{1,0:T(8,128)S(1)} fusion(f32[24,8192]{1,0:T(8,128)S(1)} %get-tuple-element.211, s32[32]{0:T(128)S(1)} %fusion.73, f32[32,8192]{1,0:T(8,128)S(1)} %reshape.339), kind=kCustom, calls=%fused_computation.2.clone.1 | custom fusion | flops 262144 | bytes 3145856 | tf_op jit(solution)/shard_map/while/body/eval_jaxpr/scatter-add | solution.py:112
  104.1 1.1 constant_dynamic-slice_fusion.5
  105.2 1.5 fusion.74
  106.7 0.9 fusion.75
  107.5 1.3 copy-done
  108.8 1.7 %convolution_bitcast_fusion.5 = f32[2,1024,128]{2,1,0:T(8,128)} fusion(bf16[1,2,64,4,128]{4,3,2,1,0:T(4,128)(2,1)S(1)} %get-tuple-element.196, f32[2,4,64,1024]{3,2,1,0:T(8,128)S(1)} %get-tuple-element.194, f32[2,4,64]{2,1,0:T(4,128)S(1)} %get-tuple-element.195), kind=kOutput, calls=%fused_computation.16.clone.1 | convolution fusion | flops 135266304 | bytes 3278848 | tf_op jit(solution)/shard_map/while/body/eval_jaxpr/qgis,qigw->qsw/dot_general | solution.py:109
  110.5 1.4 reshape.340
  111.9 2.1 %scatter_fusion.1 = f32[24,8192]{1,0:T(8,128)S(1)} fusion(f32[24,8192]{1,0:T(8,128)S(1)} %get-tuple-element.212, s32[32]{0:T(128)S(1)} %fusion.73, f32[32,8192]{1,0:T(8,128)S(1)} %reshape.340), kind=kCustom, calls=%fused_computation.3.clone.1 | custom fusion | flops 262144 | bytes 3145856 | tf_op jit(solution)/shard_map/while/body/eval_jaxpr/scatter-add | solution.py:113
  114.0 2.4 %fusion.76 = (f32[2,4,64]{2,1,0:T(4,128)S(1)}, f32[2,1024,64,4]{1,2,3,0:T(8,128)S(1)}) fusion(f32[2,4,64,1024]{3,2,1,0:T(8,128)} %copy-done, f32[2,4,64]{2,1,0:T(4,128)S(1)} %get-tuple-element.195, bf16[1,2,64,4,128]{4,3,2,1,0:T(4,128)(2,1)S(1)} %get-tuple-element.196, bf16[4,2,1024,128]{3,2,1,0:T(8,128)(2,1)} %get-tuple-element.229, s32[]{:T(128)S(6)} %copy.91), kind=kOutput, calls=%fused_computation.7.clone.1 | convolution fusion | flops 135790080 | bytes 4853764 | tf_op jit(solution)/shard_map/while/body/eval_jaxpr/qigw,qsw->qgis/dot_general | solution.py:98
  116.8 1.5 fusion.79
  118.3 1.5 fusion.78
  119.9 1.4 reshape.339
  121.3 2.1 %scatter_fusion = f32[24,8192]{1,0:T(8,128)S(1)} fusion(f32[24,8192]{1,0:T(8,128)S(1)} %get-tuple-element.211, s32[32]{0:T(128)S(1)} %fusion.73, f32[32,8192]{1,0:T(8,128)S(1)} %reshape.339), kind=kCustom, calls=%fused_computation.2.clone.1 | custom fusion | flops 262144 | bytes 3145856 | tf_op jit(solution)/shard_map/while/body/eval_jaxpr/scatter-add | solution.py:112
  124.2 0.9 reshape.280
  125.1 3.5 %all-to-all-start = ((f32[4,4,8192]{2,1,0:T(4,128)}), f32[4,4,8192]{2,1,0:T(4,128)S(1)}, u32[]{:S(2)}, u32[]{:S(2)}) async-start(f32[4,4,8192]{2,1,0:T(4,128)} %reshape.280), calls=%async_computation | async-start | bytes 1048576 | tf_op jit(solution)/shard_map/all_to_all | solution.py:129
  129.0 1.0 reshape.282
  130.0 8.9 %all-to-all-done = f32[4,4,8192]{2,1,0:T(4,128)S(1)} async-done(((f32[4,4,8192]{2,1,0:T(4,128)}), f32[4,4,8192]{2,1,0:T(4,128)S(1)}, u32[]{:S(2)}, u32[]{:S(2)}) %all-to-all-start) | async-done | bytes 524320 | tf_op jit(solution)/shard_map/all_to_all | solution.py:129
  138.9 3.5 %all-to-all-start.1 = ((f32[4,4,8192]{2,1,0:T(4,128)}), f32[4,4,8192]{2,1,0:T(4,128)S(1)}, u32[]{:S(2)}, u32[]{:S(2)}) async-start(f32[4,4,8192]{2,1,0:T(4,128)} %reshape.282), calls=%async_computation.1 | async-start | bytes 1048576 | tf_op jit(solution)/shard_map/all_to_all | solution.py:130
  142.7 0.9 fusion.30
  143.6 9.0 %all-to-all-done.1 = f32[4,4,8192]{2,1,0:T(4,128)S(1)} async-done(((f32[4,4,8192]{2,1,0:T(4,128)}), f32[4,4,8192]{2,1,0:T(4,128)S(1)}, u32[]{:S(2)}, u32[]{:S(2)}) %all-to-all-start.1) | async-done | bytes 524320 | tf_op jit(solution)/shard_map/all_to_all | solution.py:130
  153.5 4.8 %all-reduce.2 = (bf16[8,8192]{1,0:T(8,128)(2,1)S(1)}, bf16[8,8192]{1,0:T(8,128)(2,1)S(1)}) all-reduce(f32[8,8192]{1,0:T(8,128)S(1)} %fusion.30, f32[8,8192]{1,0:T(8,128)S(1)} %fusion.31), channel_id=1, replica_groups=mesh['groups'=2,'seq'=4,'head'=2,'inner'=2] {'inner'}, use_global_device_ids=true, to_apply=%region_12.14 | all-reduce | flops 131072 | bytes 786432 | tf_op jit(solution)/shard_map/psum | solution.py:138
  (95 shorter events, 13.0 us)
Async XLA Ops:
  0.6 23.3 %collective-permute-start = (bf16[512,1,128]{2,0,1:T(8,128)(2,1)}, bf16[512,1,128]{2,0,1:T(8,128)(2,1)S(1)}, u32[]{:S(2)}, u32[]{:S(2)}) collective-permute-start(bf16[512,1,128]{2,0,1:T(8,128)(2,1)} %param.13), channel_id=1, source_target_pairs={{0,4},{4,8},{8,12},{12,0},{1,5},{5,9},{9,13},{13,1},{2,6},{6,10},{... | collective-permute-start | bytes 393224 | tf_op jit(solution)/shard_map/ppermute | solution.py:56
  4.7 0.8 copy-start.3
  23.0 14.6 %copy-start.2 = (bf16[512,1,128]{2,0,1:T(8,128)(2,1)S(1)}, bf16[512,1,128]{2,0,1:T(8,128)(2,1)}, u32[]{:S(2)}) copy-start(bf16[512,1,128]{2,0,1:T(8,128)(2,1)} %param.13) | copy-start | bytes 393220
  24.0 6.8 %collective-permute-start.1 = (bf16[512,1,128]{2,0,1:T(8,128)(2,1)S(1)}, bf16[512,1,128]{2,0,1:T(8,128)(2,1)S(1)}, u32[]{:S(2)}, u32[]{:S(2)}) collective-permute-start(bf16[512,1,128]{2,0,1:T(8,128)(2,1)S(1)} %collective-permute-done), channel_id=1, source_target_pairs={{0,4},{4,8},{8,12},{12,0},{1,5},{5,9},{9,13},{13,1},{2,6},{6,10},{... | collective-permute-start | bytes 393224 | tf_op jit(solution)/shard_map/ppermute | solution.py:56
  30.8 6.8 %collective-permute-start.2 = (bf16[512,1,128]{2,0,1:T(8,128)(2,1)S(1)}, bf16[512,1,128]{2,0,1:T(8,128)(2,1)S(1)}, u32[]{:S(2)}, u32[]{:S(2)}) collective-permute-start(bf16[512,1,128]{2,0,1:T(8,128)(2,1)S(1)} %collective-permute-done.1), channel_id=1, source_target_pairs={{0,4},{4,8},{8,12},{12,0},{1,5},{5,9},{9,13},{13,1},{2,6},{6,10},{... | collective-permute-start | bytes 393224 | tf_op jit(solution)/shard_map/ppermute | solution.py:56
  47.3 1.3 copy-start
  53.8 2.4 %copy-start.1 = (f32[2,4,64,1024]{3,2,1,0:T(8,128)S(1)}, f32[2,4,64,1024]{3,2,1,0:T(8,128)}, u32[]{:S(2)}) copy-start(f32[2,4,64,1024]{3,2,1,0:T(8,128)} %copy-done) | copy-start | bytes 6291460 | tf_op jit(solution)/shard_map/while
  67.3 1.3 copy-start
  73.8 2.4 %copy-start.1 = (f32[2,4,64,1024]{3,2,1,0:T(8,128)S(1)}, f32[2,4,64,1024]{3,2,1,0:T(8,128)}, u32[]{:S(2)}) copy-start(f32[2,4,64,1024]{3,2,1,0:T(8,128)} %copy-done) | copy-start | bytes 6291460 | tf_op jit(solution)/shard_map/while
  87.4 1.3 copy-start
  93.9 2.4 %copy-start.1 = (f32[2,4,64,1024]{3,2,1,0:T(8,128)S(1)}, f32[2,4,64,1024]{3,2,1,0:T(8,128)}, u32[]{:S(2)}) copy-start(f32[2,4,64,1024]{3,2,1,0:T(8,128)} %copy-done) | copy-start | bytes 6291460 | tf_op jit(solution)/shard_map/while
  107.5 1.3 copy-start
  114.0 2.4 %copy-start.1 = (f32[2,4,64,1024]{3,2,1,0:T(8,128)S(1)}, f32[2,4,64,1024]{3,2,1,0:T(8,128)}, u32[]{:S(2)}) copy-start(f32[2,4,64,1024]{3,2,1,0:T(8,128)} %copy-done) | copy-start | bytes 6291460 | tf_op jit(solution)/shard_map/while
  125.1 13.7 %all-to-all-start = ((f32[4,4,8192]{2,1,0:T(4,128)}), f32[4,4,8192]{2,1,0:T(4,128)S(1)}, u32[]{:S(2)}, u32[]{:S(2)}) async-start(f32[4,4,8192]{2,1,0:T(4,128)} %reshape.280), calls=%async_computation | async-start | bytes 1048576 | tf_op jit(solution)/shard_map/all_to_all | solution.py:129
  138.9 13.7 %all-to-all-start.1 = ((f32[4,4,8192]{2,1,0:T(4,128)}), f32[4,4,8192]{2,1,0:T(4,128)S(1)}, u32[]{:S(2)}, u32[]{:S(2)}) async-start(f32[4,4,8192]{2,1,0:T(4,128)} %reshape.282), calls=%async_computation.1 | async-start | bytes 1048576 | tf_op jit(solution)/shard_map/all_to_all | solution.py:130
